TPU v7x, 256 devices: a whole 4x4x8 slice. The times are simulated.
256 devices in a mesh: asset: 32 (over x, z), tm: 8 (over y, core).
Axes of the slice: x: 4, y: 4, z: 8, core: 2. Of those that a mesh axis runs over, the one named last changes fastest.
Arguments:
- prices: float32 [480, 61440], P('tm', 'asset'), may hold values from -10 to 20
- sectors: int32 [61440], P('asset'), may hold values from 0 to 10, as said below
- wanted: int32 [32, 8, 32], replicated, may hold values from -1 to 14, as said below
- pair_slots: int32 [32768, 2], P(('asset', 'tm')), may hold values from 0 to 31, as said below
- pair_count: int32 [256], P(('asset', 'tm')), may hold values from 16 to 128, as said below
Outputs:
- comovement: float32 [32768, 4, 2, 128], P(('asset', 'tm'))
Inputs may be any that keep to these rules, and one draw needn't show every extreme that they name: Every one of the 11 sectors holds at least one series. `wanted`: every device needs a block from at least one column; in every draw some device needs one from every column. `pair_slots`: both columns of a pair row of device g = d * 8 + t have wanted[d, t, column] >= 0. `pair_count`: the rows in use are a device's first ones; some device uses all 128.
All inputs are finite; a program needn't handle non-finite values.
Results may differ from a plain program's by a relative error of at most 0.00046.
Values may be sent and summed in bfloat16 or wider, within the bound.
A program may use at most 128 MiB of HBM per device.

v0:
```python
import jax
import jax.numpy as jnp
from jax import lax
from jax.sharding import PartitionSpec as P

BLK = 128
SECT = 11


epsilon = 1e-06
highest = lax.Precision.HIGHEST


def shifted(block, axis, distance):
    devices = range(lax.axis_size(axis))
    route = [(i - distance, i) for i in devices if i - distance in devices]
    return lax.ppermute(block, axis, route)


def copy_for_each(array, axis):
    devices = lax.axis_size(axis)
    return lax.all_to_all(
        jnp.broadcast_to(array[None], (devices, *array.shape)), axis, 0, 0, tiled=True
    )


def taken_together(array, axis):
    return copy_for_each(array, axis).sum(axis=0)


def in_one(arrays, axis):
    ends = [0]
    for a in arrays:
        ends.append(ends[-1] + a.size)
    subtotal = taken_together(jnp.concatenate([a.ravel() for a in arrays]), axis)
    return tuple((subtotal[b:e].reshape(a.shape) for a, b, e in zip(arrays, ends, ends[1:])))


def split_up(array, dim, devices):
    before, after = (array.shape[:dim], array.shape[dim + 1 :])
    return jnp.moveaxis(array.reshape(*before, devices, -1, *after), dim, 0)


def in_order(parts, dim):
    parts = jnp.moveaxis(parts, 0, dim)
    lengths = parts.shape
    return parts.reshape(*lengths[:dim], lengths[dim] * lengths[dim + 1], *lengths[dim + 2 :])


def exchange_both(array, axis, axes, splits, concats):
    sizes = [lax.axis_size(a) for a in axes]
    parts = split_up(array, splits[0], sizes[0])
    parts = jnp.moveaxis(split_up(parts, splits[1] + 1, sizes[1]), 0, 1)
    inside = parts.shape[2:]
    parts = parts.reshape(-1, *inside)
    parts = lax.all_to_all(parts, axis, split_axis=0, concat_axis=0, tiled=True)
    parts = in_order(parts.reshape(*sizes, *inside), concats[0] + 1)
    return in_order(parts, concats[1])


def moments(held, opening, closing):
    portion = held[opening:closing].astype(jnp.float32)
    average = jnp.sum(portion, axis=0) / (closing - opening)
    second = jnp.sum(portion * portion, axis=0) / (closing - opening)
    return (average, lax.rsqrt(second - average * average + epsilon))


def products(first_block, second_block, opening, closing):
    return jnp.einsum(
        "pti,ptj->pij",
        first_block[:, opening:closing],
        second_block[:, opening:closing],
        preferred_element_type=jnp.float32,
    )


def on_device(prices, sectors, wanted, pair_slots, pair_count):
    stretch = prices.shape[0]
    column_index = lax.axis_index("asset")
    stretch_index = lax.axis_index("tm")
    previous = shifted(prices[stretch - 1 :], "tm", 1)
    earlier = jnp.concatenate([previous, prices[: stretch - 1]], axis=0)
    minute = stretch_index * stretch + lax.iota(jnp.int32, stretch)
    returns = jnp.where((minute > 0)[:, None], prices - earlier, jnp.zeros((), jnp.float32))
    labels = lax.iota(jnp.int32, SECT)
    member = (sectors[:, None] == labels[None, :]).astype(jnp.float32)
    totals, members = in_one(
        (jnp.dot(returns, member, precision=highest), jnp.sum(member, axis=0)), "asset"
    )
    sector_mean = totals / members
    neutral = (returns - jnp.dot(sector_mean, member.T, precision=highest)).astype(jnp.bfloat16)
    count_blocks = prices.shape[1] // BLK
    blocks = neutral.reshape(stretch, count_blocks, BLK)
    requests = lax.dynamic_index_in_dim(wanted, column_index, 2, keepdims=False)
    block_ids = lax.iota(jnp.int32, count_blocks)
    selector = (requests[:, :, None] == block_ids[None, None, :]).astype(jnp.bfloat16)
    outgoing = jnp.einsum(
        "dtb,mbj->mdtj", selector, blocks, preferred_element_type=jnp.float32
    ).astype(jnp.bfloat16)
    arrived = exchange_both(outgoing, ("asset", "tm"), ("asset", "tm"), (1, 2), (1, 0))
    series = arrived.reshape(arrived.shape[0], arrived.shape[1], BLK)
    time_all = series.shape[0]
    stride = time_all // 16
    length = 13 * time_all // 16
    stats = [moments(series, window * stride, window * stride + length) for window in range(4)]
    center = jnp.stack([entry[0] for entry in stats], axis=1)
    inverse = jnp.stack([entry[1] for entry in stats], axis=1)
    by_column = jnp.transpose(series, (1, 0, 2))
    first_ids = pair_slots[:, 0]
    second_ids = pair_slots[:, 1]
    first_block = jnp.take(by_column, first_ids, axis=0)
    second_block = jnp.take(by_column, second_ids, axis=0)
    center_first = jnp.take(center, first_ids, axis=0)
    center_second = jnp.take(center, second_ids, axis=0)
    inverse_first = jnp.take(inverse, first_ids, axis=0)
    inverse_second = jnp.take(inverse, second_ids, axis=0)
    windows = [
        products(first_block, second_block, window * stride, window * stride + length)
        for window in range(4)
    ]
    summaries = []
    for window in range(4):
        correlation = (
            windows[window] / length
            - center_first[:, window, :, None] * center_second[:, window, None, :]
        )
        correlation = (
            correlation * inverse_first[:, window, :, None] * inverse_second[:, window, None, :]
        )
        square = length * correlation * correlation
        summaries.append(jnp.stack([jnp.mean(square, axis=2), jnp.mean(square, axis=1)], axis=1))
    summary = jnp.stack(summaries, axis=1)
    in_use = lax.iota(jnp.int32, pair_slots.shape[0]) < pair_count[0]
    return jnp.where(in_use[:, None, None, None], summary, jnp.zeros((), jnp.float32))


def solution(mesh):
    placed = (P("tm", "asset"), P("asset"), P(), P(("asset", "tm"), None), P(("asset", "tm")))
    return jax.shard_map(
        on_device,
        mesh=mesh,
        in_specs=placed,
        out_specs=P(("asset", "tm"), None, None, None),
        check_vma=False,
    )
```

profile of v0, /device:TPU:1, one launch (start us, length us, event | category | flops | bytes accessed | tf_op | source)
XLA Modules:
  0.0 275.5 jit_solution(9625171343272482559)
XLA Ops:
  0.0 0.9 slice.110
  0.9 4.6 %collective-permute-start = (f32[1,1920]{1,0:T(1,128)S(1)}, f32[1,1920]{1,0:T(1,128)S(1)}, u32[]{:S(2)}, u32[]{:S(2)}) collective-permute-start(f32[1,1920]{1,0:T(1,128)S(1)} %slice.110), channel_id=1, source_target_pairs={{0,1},{1,2},{2,3},{3,4},{4,5},{5,6},{6,7},{8,9},{9,10},{10,11},{11... | collective-permute-start | bytes 23048 | tf_op jit(solution)/shard_map/ppermute | solution.py:17
  5.5 0.8 convert_reduce_fusion.4
  6.3 1.7 fusion.27
  8.9 11.0 %all-to-all-start = ((f32[32,1,671]{2,1,0:T(1,128)}), f32[32,1,671]{2,1,0:T(1,128)S(1)}, u32[]{:S(2)}, u32[]{:S(2)}) async-start(f32[32,1,671]{2,1,0:T(1,128)} %broadcast_in_dim.58), calls=%async_computation | async-start | bytes 196608 | tf_op jit(solution)/shard_map/all_to_all | solution.py:22
  20.2 9.2 %all-to-all-done = f32[32,1,671]{2,1,0:T(1,128)S(1)} async-done(((f32[32,1,671]{2,1,0:T(1,128)}), f32[32,1,671]{2,1,0:T(1,128)S(1)}, u32[]{:S(2)}, u32[]{:S(2)}) %all-to-all-start) | async-done | bytes 85920 | tf_op jit(solution)/shard_map/all_to_all | solution.py:22
  29.7 1.6 fusion.24
  31.5 1.2 convert_bitcast_fusion
  32.7 3.9 %copy.128 = bf16[32,8,60,1,1,128]{5,1,0,2,4,3:T(8,128)(2,1)S(1)} copy(bf16[32,8,60,1,1,128]{5,0,1,2,4,3:T(8,128)(2,1)S(1)} %convert_bitcast_fusion) | data formatting | bytes 7864320 | tf_op jit(solution)/shard_map/transpose;transpose | solution.py:53
  36.6 4.5 %copy.105 = bf16[256,60,1,1,128]{4,1,3,2,0:T(8,128)(2,1)} copy(bf16[256,60,1,1,128]{4,0,1,3,2:T(8,128)(2,1)S(1)} %bitcast.123) | data formatting | bytes 7864320 | tf_op jit(solution)/shard_map/reshape | solution.py:55
  41.2 9.4 %all-to-all-start.1 = ((bf16[256,60,1,1,128]{4,1,3,2,0:T(8,128)(2,1)}), bf16[256,60,1,1,128]{4,1,3,2,0:T(8,128)(2,1)}, u32[]{:S(2)}, u32[]{:S(2)}) async-start(bf16[256,60,1,1,128]{4,1,3,2,0:T(8,128)(2,1)} %copy.105), calls=%async_computation.1 | async-start | bytes 8388608 | tf_op jit(solution)/shard_map/all_to_all | solution.py:56
  51.8 96.0 %all-to-all-done.1 = bf16[256,60,1,1,128]{4,1,3,2,0:T(8,128)(2,1)} async-done(((bf16[256,60,1,1,128]{4,1,3,2,0:T(8,128)(2,1)}), bf16[256,60,1,1,128]{4,1,3,2,0:T(8,128)(2,1)}, u32[]{:S(2)}, u32[]{:S(2)}) %all-to-all-start.1) | async-done | bytes 3932192 | tf_op jit(solution)/shard_map/all_to_all | solution.py:56
  147.9 4.7 %copy.127 = bf16[256,60,1,1,128]{4,0,1,3,2:T(8,128)(2,1)S(1)} copy(bf16[256,60,1,1,128]{4,1,3,2,0:T(8,128)(2,1)} %all-to-all-done.1) | data formatting | bytes 7864320 | tf_op jit(solution)/shard_map/all_to_all | solution.py:56
  153.3 1.9 copy-done.2
  155.2 3.4 %convert_reduce_fusion.3 = (f32[32,128]{1,0:T(8,128)S(1)}, f32[32,128]{1,0:T(8,128)S(1)}, f32[32,128]{1,0:T(8,128)S(1)}, f32[32,128]{1,0:T(8,128)S(1)}, f32[32,1...) fusion(bf16[480,32,128]{2,1,0:T(8,128)(2,1)S(1)} %bitcast.121), kind=kLoop, calls=%fused_computation.31 | loop fusion | flops 25526272 | bytes 12910592 | tf_op jit(solution)/shard_map/reduce_sum | solution.py:63
  161.8 5.5 %copy.126 = bf16[480,32,128]{2,0,1:T(8,128)(2,1)} copy(bf16[480,32,128]{2,1,0:T(8,128)(2,1)} %bitcast.122) | data formatting | bytes 7864320 | tf_op jit(solution)/shard_map/reshape;reshape;reshape | solution.py:101
  167.3 10.3 %gather_fusion = bf16[128,480,128]{2,1,0:T(8,128)(2,1)} fusion(bf16[32,480,128]{2,1,0:T(8,128)(2,1)} %bitcast.119, s32[1024]{0:T(1024)S(1)} %pad_clamp_fusion.1), kind=kCustom, calls=%fused_computation.clone | custom fusion | bytes 31457792 | tf_op jit(solution)/shard_map/jit(_take)/gather | solution.py:111
  177.5 10.3 %gather_fusion.1 = bf16[128,480,128]{2,1,0:T(8,128)(2,1)} fusion(bf16[32,480,128]{2,1,0:T(8,128)(2,1)} %bitcast.120, s32[1024]{0:T(1024)S(1)} %pad_clamp_fusion), kind=kCustom, calls=%fused_computation.2.clone | custom fusion | bytes 31457792 | tf_op jit(solution)/shard_map/jit(_take)/gather | solution.py:112
  189.0 17.3 %broadcast_select_fusion = (bf16[128,480,128]{2,1,0:T(8,128)(2,1)S(1)}, bf16[128,480,128]{2,1,0:T(8,128)(2,1)}) fusion(bf16[128,480,128]{2,1,0:T(8,128)(2,1)} %gather_fusion.1, pred[128]{0:T(512)(128)(4,1)S(1)} %get-tuple-element.43, bf16[128,480,128]{2,1,0:T(8,128)(2,1)} %gather_fusion, pred[128]{0:T(512)(128)(4,1)S(1)} %get-tuple-element.23), kind=kLoop, calls=%fused_computation.6 | loop fusion | flops 15728640 | bytes 62914816 | tf_op jit(solution)/shard_map/jit(_take)/select_n | solution.py:112
  206.4 14.7 %fusion.17 = (f32[128,128]{1,0:T(8,128)S(1)}, f32[128,128]{1,0:T(8,128)S(1)}) fusion(f32[128,128]{1,0:T(8,128)S(1)} %bitcast.144, f32[128,128]{1,0:T(8,128)S(1)} %bitcast.141, f32[128,128]{1,0:T(8,128)S(1)} %bitcast.143, f32[128,128]{1,0:T(8,128)S(1)} %bitcast.139, bf16[128,480,128]{2,1,0:T(8,128)(2,1)S(1)} %get-tuple-element.57, ...), kind=kOutput, calls=%fused_computation.37 | convolution fusion | flops 1654620160 | bytes 26083328 | tf_op jit(solution)/shard_map/pti,ptj->pij/dot_general | solution.py:69
  221.2 17.5 %fusion.19 = (f32[128,128]{1,0:T(8,128)S(1)}, f32[128,128]{1,0:T(8,128)S(1)}) fusion(f32[128,128]{1,0:T(8,128)S(1)} %bitcast.142, f32[128,128]{1,0:T(8,128)S(1)} %bitcast.137, f32[128,128]{1,0:T(8,128)S(1)} %bitcast.140, f32[128,128]{1,0:T(8,128)S(1)} %bitcast.135, bf16[128,480,128]{2,1,0:T(8,128)(2,1)S(1)} %get-tuple-element.57, ...), kind=kOutput, calls=%fused_computation.39 | convolution fusion | flops 1654620160 | bytes 26083328 | tf_op jit(solution)/shard_map/pti,ptj->pij/dot_general | solution.py:69
  238.9 17.6 %fusion.21 = (f32[128,128]{1,0:T(8,128)S(1)}, f32[128,128]{1,0:T(8,128)S(1)}) fusion(f32[128,128]{1,0:T(8,128)S(1)} %bitcast.138, f32[128,128]{1,0:T(8,128)S(1)} %bitcast.134, f32[128,128]{1,0:T(8,128)S(1)} %bitcast.136, f32[128,128]{1,0:T(8,128)S(1)} %bitcast.132, bf16[128,480,128]{2,1,0:T(8,128)(2,1)S(1)} %get-tuple-element.57, ...), kind=kOutput, calls=%fused_computation.41 | convolution fusion | flops 1654620160 | bytes 26083328 | tf_op jit(solution)/shard_map/pti,ptj->pij/dot_general | solution.py:69
  256.7 17.5 %fusion.23 = (f32[128,128]{1,0:T(8,128)S(1)}, f32[128,128]{1,0:T(8,128)S(1)}) fusion(f32[128,128]{1,0:T(8,128)S(1)} %bitcast.133, f32[128,128]{1,0:T(8,128)S(1)} %bitcast.130, f32[128,128]{1,0:T(8,128)S(1)} %bitcast.131, f32[128,128]{1,0:T(8,128)S(1)} %bitcast.129, bf16[128,480,128]{2,1,0:T(8,128)(2,1)S(1)} %get-tuple-element.57, ...), kind=kOutput, calls=%fused_computation.43 | convolution fusion | flops 1654620160 | bytes 26083328 | tf_op jit(solution)/shard_map/pti,ptj->pij/dot_general | solution.py:69
  274.4 1.1 maximum_select_fusion
  (58 shorter events, 7.7 us)
Async XLA Ops:
  0.0 19.9 %copy-start = (s32[32,8,32]{2,1,0:T(8,128)S(1)}, s32[32,8,32]{2,1,0:T(8,128)}, u32[]{:S(2)}) copy-start(s32[32,8,32]{2,1,0:T(8,128)} %param.11) | copy-start | bytes 98308
  0.9 5.4 %collective-permute-start = (f32[1,1920]{1,0:T(1,128)S(1)}, f32[1,1920]{1,0:T(1,128)S(1)}, u32[]{:S(2)}, u32[]{:S(2)}) collective-permute-start(f32[1,1920]{1,0:T(1,128)S(1)} %slice.110), channel_id=1, source_target_pairs={{0,1},{1,2},{2,3},{3,4},{4,5},{5,6},{6,7},{8,9},{9,10},{10,11},{11... | collective-permute-start | bytes 23048 | tf_op jit(solution)/shard_map/ppermute | solution.py:17
  8.9 20.5 %all-to-all-start = ((f32[32,1,671]{2,1,0:T(1,128)}), f32[32,1,671]{2,1,0:T(1,128)S(1)}, u32[]{:S(2)}, u32[]{:S(2)}) async-start(f32[32,1,671]{2,1,0:T(1,128)} %broadcast_in_dim.58), calls=%async_computation | async-start | bytes 196608 | tf_op jit(solution)/shard_map/all_to_all | solution.py:22
  36.6 15.2 %copy-start.3 = (s32[128,2]{0,1:T(2,128)S(1)}, s32[128,2]{0,1:T(2,128)}, u32[]{:S(2)}) copy-start(s32[128,2]{0,1:T(2,128)} %param.12) | copy-start | bytes 3076
  41.2 106.7 %all-to-all-start.1 = ((bf16[256,60,1,1,128]{4,1,3,2,0:T(8,128)(2,1)}), bf16[256,60,1,1,128]{4,1,3,2,0:T(8,128)(2,1)}, u32[]{:S(2)}, u32[]{:S(2)}) async-start(bf16[256,60,1,1,128]{4,1,3,2,0:T(8,128)(2,1)} %copy.105), calls=%async_computation.1 | async-start | bytes 8388608 | tf_op jit(solution)/shard_map/all_to_all | solution.py:56
  153.3 1.9 copy-start.2
  256.7 17.7 %copy-start.4 = (pred[128]{0:T(512)(128)(4,1)S(1)}, pred[128]{0:T(512)(128)(4,1)}, u32[]{:S(2)}) copy-start(pred[128]{0:T(512)(128)(4,1)} %iota_compare_fusion.4) | copy-start | bytes 388
  256.7 18.8 %copy-start.1 = (s32[32,8,32]{2,1,0:T(8,128)S(1)}, s32[32,8,32]{2,1,0:T(8,128)}, u32[]{:S(2)}) copy-start(s32[32,8,32]{2,1,0:T(8,128)} %param.11) | copy-start | bytes 98308
where the time goes:
time: 276 us
  waiting for transfers between devices  105 us (38%)
  matrix products  71.8 us (26%)
  local copies, waits for them, and re-layouts  48.3 us (18%)
  starting transfers between devices  25 us (9%)
  other arithmetic  24.1 us (9%)
    all_to_all x1, waiting for transfers between devices, exchange_both(): parts = lax.all_to_all(parts, axis, split_axis=0, concat_axis=0, tiled=True)  96 us
    dot_general x4, matrix products, products(): jnp.einsum('pti,ptj->pij', first_block[:, opening:closing], second_block[...  67.3 us
    select_n x1, other arithmetic, on_device(): second_block = jnp.take(by_column, second_ids, axis=0)  17.3 us
    all_to_all x1, starting transfers between devices, copy_for_each(): lax.all_to_all(jnp.broadcast_to(array[None], (devices, *array.shape)), ax...  11 us
    gather x1, local copies, waits for them, and re-layouts, on_device(): second_block = jnp.take(by_column, second_ids, axis=0)  10.3 us
    gather x1, local copies, waits for them, and re-layouts, on_device(): first_block = jnp.take(by_column, first_ids, axis=0)  10.3 us
    all_to_all x1, starting transfers between devices, exchange_both(): parts = lax.all_to_all(parts, axis, split_axis=0, concat_axis=0, tiled=True)  9.38 us
    all_to_all x1, waiting for transfers between devices, copy_for_each(): lax.all_to_all(jnp.broadcast_to(array[None], (devices, *array.shape)), ax...  9.22 us
  transfers between devices with their start and end apart: 3, of which 2 were waited for; matrix products, arithmetic and copies ran while one was open for 1% of the time, Pallas kernels for 0%

commit v1 on v0

v1 whole, which is shorter than its diff:
```python
import functools

import jax
import jax.numpy as jnp
from jax import lax
from jax.experimental import pallas as pl
from jax.experimental.pallas import tpu as pltpu
from jax.sharding import PartitionSpec as P

BLK = 128
SECT = 11
NX, NZ, NY, NC = 4, 8, 4, 2
NA, NT = NX * NZ, NY * NC
ROWS = 64
MINUTES = 60
HALF = 30
WIN = 390
NW = 4
MESH = pl.DeviceIdType.MESH

epsilon = 1e-06
highest = lax.Precision.HIGHEST


def shifted(block, axis, distance):
    devices = range(lax.axis_size(axis))
    route = [(i - distance, i) for i in devices if i - distance in devices]
    return lax.ppermute(block, axis, route)


def total_kernel(message, total, slots, send_sem, recv_sem):
    d = lax.axis_index("asset")
    t = lax.axis_index("tm")
    barrier = pltpu.get_barrier_semaphore()
    for k in range(1, NA):
        pl.semaphore_signal(barrier, inc=1, device_id=((d + k) % NA, t), device_id_type=MESH)
    pl.semaphore_wait(barrier, NA - 1)
    copies = []
    for k in range(1, NA):
        copy = pltpu.make_async_remote_copy(
            src_ref=message,
            dst_ref=slots.at[k],
            send_sem=send_sem.at[k],
            recv_sem=recv_sem.at[k],
            device_id=((d + k) % NA, t),
            device_id_type=MESH,
        )
        copy.start()
        copies.append(copy)
    subtotal = message[...]
    for k, copy in enumerate(copies):
        copy.wait_recv()
        subtotal = subtotal + slots[k + 1]
    total[...] = subtotal
    for copy in copies:
        copy.wait_send()


def summed(message):
    return pl.pallas_call(
        total_kernel,
        out_shape=jax.ShapeDtypeStruct(message.shape, message.dtype),
        in_specs=[pl.BlockSpec(memory_space=pltpu.VMEM)],
        out_specs=pl.BlockSpec(memory_space=pltpu.VMEM),
        scratch_shapes=[
            pltpu.VMEM((NA, *message.shape), message.dtype),
            pltpu.SemaphoreType.DMA((NA,)),
            pltpu.SemaphoreType.DMA((NA,)),
        ],
        compiler_params=pltpu.CompilerParams(collective_id=0, has_side_effects=True),
    )(message)


ORDER = (0, 1, 7, 2, 6, 3, 5, 4)
FIRST_HALF = 8


def exchange_kernel(
    requests, blocks, out, g1, g2, g3, g4, g5, g6, g7, picked, relay,
    z_send, z_recv, x_send, x_recv, y_send, y_recv, own_sem,
):
    d = lax.axis_index("asset")
    t = lax.axis_index("tm")
    x, z, y, c = d // NZ, d % NZ, t // NC, t % NC
    gathered = (blocks, g1, g2, g3, g4, g5, g6, g7)
    count = blocks.shape[0]

    def at_x(k):
        return ((x + k) % NX) * NZ + z, t

    def at_z(k):
        return x * NZ + (z + k + NZ) % NZ, t

    others = [(dy, dc) for dy in (1, 3, 2, 0) for dc in (0, 1) if (dy, dc) != (0, 0)]

    def at_y(k, sign):
        dy, dc = others[k]
        return d, ((y + sign * dy + NY) % NY) * NC + (c + dc) % NC

    barrier = pltpu.get_barrier_semaphore()
    peers = [at_z(1), at_z(-1)] + [at_x(k) for k in range(1, NX)]
    peers += [at_y(k, 1) for k in range(len(others))]
    for peer in peers:
        pl.semaphore_signal(barrier, inc=1, device_id=peer, device_id_type=MESH)

    pending = []

    def along_z(source, target, number, first, size, step):
        copy = pltpu.make_async_remote_copy(
            src_ref=gathered[source].at[pl.ds(first, size)],
            dst_ref=gathered[target].at[pl.ds(first, size)],
            send_sem=z_send.at[number],
            recv_sem=z_recv.at[number],
            device_id=at_z(step),
            device_id_type=MESH,
        )
        copy.start()
        pending.append(copy)
        return copy

    def pick(j):
        for k in (1, 3, 2, 0):
            def one(i, _):
                block = gathered[j][requests[(j * NX + k) * NT + i]]
                if k == 0:
                    relay[j, i, 0] = block
                else:
                    picked[j, k - 1, i] = block
                return 0
            lax.fori_loop(0, NT, one, 0)

    def along_x(j):
        copies = []
        for k in (1, 3, 2):
            copy = pltpu.make_async_remote_copy(
                src_ref=picked.at[j, k - 1],
                dst_ref=relay.at[j, :, k],
                send_sem=x_send.at[j, k],
                recv_sem=x_recv.at[j, k],
                device_id=at_x(k),
                device_id_type=MESH,
            )
            copy.start()
            copies.append(copy)
        pending.extend(copies)
        return copies

    def along_y(j, arriving):
        for copy in arriving:
            copy.wait_recv()
        copies = []
        for k in range(len(others)):
            target = at_y(k, 1)
            copy = pltpu.make_async_remote_copy(
                src_ref=relay.at[j, target[1]],
                dst_ref=out.at[j, t],
                send_sem=y_send.at[j, k],
                recv_sem=y_recv.at[j, k],
                device_id=target,
                device_id_type=MESH,
            )
            copy.start()
            copies.append(copy)
        pending.extend(copies)
        own = pltpu.make_async_copy(relay.at[j, t], out.at[j, t], own_sem.at[j])
        own.start()
        return copies, own

    pl.semaphore_wait(barrier, len(peers))
    arrivals = {}
    arrivals[1] = [along_z(0, 1, 1, 0, count, 1)]
    arrivals[7] = [along_z(0, 7, 7, 0, count, -1)]
    crossing = {}
    landing = []
    previous = None
    for j in ORDER:
        for copy in arrivals.get(j, ()):
            copy.wait_recv()
        if j in (1, 2):
            arrivals[j + 1] = [along_z(j, j + 1, j + 1, 0, count, 1)]
        if j in (7, 6):
            arrivals[j - 1] = [along_z(j, j - 1, j - 1, 0, count, -1)]
        if j == 3:
            arrivals[4] = [along_z(3, 4, 4, 0, FIRST_HALF, 1)]
        if j == 5:
            arrivals[4].append(along_z(5, 4, 0, FIRST_HALF, count - FIRST_HALF, -1))
        pick(j)
        crossing[j] = along_x(j)
        if previous is not None:
            landing.append(along_y(previous, crossing[previous]))
        previous = j
    landing.append(along_y(previous, crossing[previous]))
    for copies, own in landing:
        for copy in copies:
            copy.wait_recv()
        own.wait()
    for copy in pending:
        copy.wait_send()


def exchanged(requests, blocks):
    count = blocks.shape[0]
    block = blocks.shape[1:]
    gathered = [pltpu.VMEM((count, *block), blocks.dtype) for _ in range(NZ - 1)]
    return pl.pallas_call(
        exchange_kernel,
        out_shape=jax.ShapeDtypeStruct((NZ, NT, NX, *block), blocks.dtype),
        in_specs=[
            pl.BlockSpec(memory_space=pltpu.SMEM),
            pl.BlockSpec(memory_space=pltpu.VMEM),
        ],
        out_specs=pl.BlockSpec(memory_space=pl.ANY),
        scratch_shapes=gathered
        + [
            pltpu.VMEM((NZ, NX - 1, NT, *block), blocks.dtype),
            pltpu.VMEM((NZ, NT, NX, *block), blocks.dtype),
            pltpu.SemaphoreType.DMA((NZ,)),
            pltpu.SemaphoreType.DMA((NZ,)),
            pltpu.SemaphoreType.DMA((NZ, NX)),
            pltpu.SemaphoreType.DMA((NZ, NX)),
            pltpu.SemaphoreType.DMA((NZ, NT)),
            pltpu.SemaphoreType.DMA((NZ, NT)),
            pltpu.SemaphoreType.DMA((NZ,)),
        ],
        compiler_params=pltpu.CompilerParams(
            collective_id=1, has_side_effects=True, vmem_limit_bytes=40 * 2**20
        ),
    )(requests, blocks)


def three_parts(value):
    high = value.astype(jnp.bfloat16).astype(jnp.float32)
    rest = value - high
    middle = rest.astype(jnp.bfloat16).astype(jnp.float32)
    low = (rest - middle).astype(jnp.bfloat16).astype(jnp.float32)
    return high, middle, low


def pair_kernel(slots, used, held, out, left, right, inverse, spread, columns, product0, product1):
    row8 = lax.broadcasted_iota(jnp.int32, (8, BLK), 0)
    row = lax.broadcasted_iota(jnp.int32, (ROWS, BLK), 0)

    def prepare(slot, _):
        j, k = slot // NX, slot % NX
        chunk = [held[j, i, k].astype(jnp.float32) for i in range(NT)]
        zero = jnp.zeros((ROWS, BLK), jnp.float32)
        early = {i: jnp.where(row < HALF, chunk[i], zero) for i in (6, 7)}
        late = {i: jnp.where(row < HALF, zero, chunk[i]) for i in (0, 1)}
        kept = [
            [chunk[0], chunk[1]] + chunk[2:6] + [early[6], zero],
            [late[0], chunk[1]] + chunk[2:6] + [chunk[6], zero],
            [zero, chunk[1]] + chunk[2:6] + [chunk[6], early[7]],
            [zero, late[1]] + chunk[2:6] + [chunk[6], chunk[7]],
        ]

        def folded(a):
            return jnp.sum(a.reshape(ROWS // 8, 8, BLK), axis=0)

        def both(a):
            return folded(a), folded(a * a)

        middle = [folded(chunk[2] + chunk[3] + chunk[4] + chunk[5])]
        middle.append(folded(sum(chunk[i] * chunk[i] for i in range(2, 6))))
        ends = {}
        sums, weights = [], []
        for w in range(NW):
            first, second = middle
            for i in (0, 1, 6, 7):
                part = kept[w][i]
                if part is zero:
                    continue
                if id(part) not in ends:
                    ends[id(part)] = both(part)
                first = first + ends[id(part)][0]
                second = second + ends[id(part)][1]
            first = jnp.sum(first, axis=0, keepdims=True)
            second = jnp.sum(second, axis=0, keepdims=True)
            center = first / WIN
            variance = second / WIN - center * center
            sums.append(first)
            weights.append(1.0 / (variance + epsilon))
        inverse[slot] = jnp.concatenate(weights + weights, axis=0)
        for w in range(NW):
            spread[slot, w] = jnp.transpose(jnp.broadcast_to(weights[w], (BLK, BLK)))

        def with_rows(tail, values):
            for n, value in enumerate(values):
                tail = jnp.where(row8 == 4 + n, jnp.broadcast_to(value, (8, BLK)), tail)
            return tail

        edge = ROWS - 8
        whole = list(chunk)
        for w in range(NW):
            h, m, l = three_parts(-sums[w])
            lefts = [h, h, m, h, l, m, m, l]
            h, m, l = three_parts(sums[w] / WIN)
            rights = [h, m, h, l, h, m, l, m]
            for n in range(2):
                i = 2 * w + n
                part = slice(4 * n, 4 * n + 4)
                whole[i] = jnp.concatenate(
                    [whole[i][:edge], with_rows(whole[i][edge:], lefts[part])], axis=0
                )
                kept[w][i] = jnp.concatenate(
                    [kept[w][i][:edge], with_rows(kept[w][i][edge:], rights[part])], axis=0
                )
            for i in range(NT):
                right[slot, pl.ds(i * ROWS, ROWS), pl.ds(w * BLK, BLK)] = kept[w][i].astype(
                    jnp.bfloat16
                )
        for i in range(0, NT, 2):
            two = jnp.concatenate([whole[i], whole[i + 1]], axis=0)
            left[slot, :, pl.ds(i * ROWS, 2 * ROWS)] = jnp.transpose(two).astype(jnp.bfloat16)
        return 0

    lax.fori_loop(0, NA, prepare, 0)

    pairs = out.shape[0]
    group = BLK // NW
    lane = lax.broadcasted_iota(jnp.int32, (BLK, BLK), 1)
    scale = 1.0 / (WIN * BLK)

    def multiply(p, product):
        a, b = slots[p, 0], slots[p, 1]
        product[...] = jnp.dot(left[a], right[b], preferred_element_type=jnp.float32)

    def reduce(p, product):
        a, b = slots[p, 0], slots[p, 1]
        within = lax.rem(p, group) * NW
        keep = columns[...]
        rows = []
        for w in range(NW):
            value = product[:, pl.ds(w * BLK, BLK)]
            scaled = value * value * spread[a, w]
            weight = inverse[b, pl.ds(w, 1)]
            over_j = jnp.sum(scaled * weight, axis=1, keepdims=True) * scale
            over_i = jnp.sum(scaled, axis=0, keepdims=True) * (weight * scale)
            keep = jnp.where(lane == within + w, over_j, keep)
            rows.append(jnp.where(p < used[0], over_i, 0.0))
        columns[...] = keep
        out[p] = jnp.concatenate([r for over_i in rows for r in (over_i, over_i)], axis=0)

    def block(n, _):
        columns[...] = jnp.zeros_like(columns)

        def two(m, _):
            p = n * group + 2 * m
            multiply(p + 1, product1)
            reduce(p, product0)
            multiply(jnp.minimum(p + 2, pairs - 1), product0)
            reduce(p + 1, product1)
            return 0

        lax.fori_loop(0, group // 2, two, 0)
        turned = jnp.transpose(columns[...])
        number = lax.broadcasted_iota(jnp.int32, (BLK, BLK), 0) // NW + n * group
        turned = jnp.where(number < used[0], turned, 0.0).reshape(group, NW, BLK)
        for w in range(NW):
            out[pl.ds(n * group, group), 2 * w, :] = turned[:, w, :]
        return 0

    multiply(0, product0)
    lax.fori_loop(0, pairs // group, block, 0)


def correlated(slots, used, held):
    pairs = slots.shape[0]
    minutes = NT * ROWS
    return pl.pallas_call(
        pair_kernel,
        out_shape=jax.ShapeDtypeStruct((pairs, 2 * NW, BLK), jnp.float32),
        in_specs=[
            pl.BlockSpec(memory_space=pltpu.SMEM),
            pl.BlockSpec(memory_space=pltpu.SMEM),
            pl.BlockSpec(memory_space=pltpu.VMEM),
        ],
        out_specs=pl.BlockSpec(memory_space=pltpu.VMEM),
        scratch_shapes=[
            pltpu.VMEM((NA, BLK, minutes), jnp.bfloat16),
            pltpu.VMEM((NA, minutes, NW * BLK), jnp.bfloat16),
            pltpu.VMEM((NA, 8, BLK), jnp.float32),
            pltpu.VMEM((NA, NW, BLK, BLK), jnp.float32),
            pltpu.VMEM((BLK, BLK), jnp.float32),
            pltpu.VMEM((BLK, NW * BLK), jnp.float32),
            pltpu.VMEM((BLK, NW * BLK), jnp.float32),
        ],
        compiler_params=pltpu.CompilerParams(vmem_limit_bytes=56 * 2**20),
    )(slots, used, held)


def on_device(prices, sectors, wanted, pair_slots, pair_count):
    stretch = prices.shape[0]
    column_index = lax.axis_index("asset")
    stretch_index = lax.axis_index("tm")
    x, z = column_index // NZ, column_index % NZ
    previous = shifted(prices[stretch - 1 :], "tm", 1)
    earlier = jnp.concatenate([previous, prices[: stretch - 1]], axis=0)
    minute = stretch_index * stretch + lax.iota(jnp.int32, stretch)
    returns = jnp.where((minute > 0)[:, None], prices - earlier, jnp.zeros((), jnp.float32))
    labels = lax.iota(jnp.int32, SECT)
    member = (sectors[:, None] == labels[None, :]).astype(jnp.float32)
    totals = jnp.dot(returns, member, precision=highest)
    members = jnp.sum(member, axis=0)
    message = jnp.concatenate([totals.ravel(), members])
    message = jnp.pad(message, (0, 8 * BLK - message.size)).reshape(8, BLK)
    message = summed(message).ravel()
    totals = message[: stretch * SECT].reshape(stretch, SECT)
    members = message[stretch * SECT : (stretch + 1) * SECT]
    sector_mean = totals / members
    neutral = (returns - jnp.dot(sector_mean, member.T, precision=highest)).astype(jnp.bfloat16)
    count = prices.shape[1] // BLK
    neutral = jnp.pad(neutral, ((0, ROWS - stretch), (0, 0)))
    blocks = jnp.transpose(neutral.reshape(ROWS, count, BLK), (1, 0, 2))

    table = wanted.reshape(NX, NZ, NT, NX, NZ)
    table = lax.dynamic_index_in_dim(table, z, 1, keepdims=False)
    table = lax.dynamic_index_in_dim(table, x, 2, keepdims=False)
    from_z = (z - lax.iota(jnp.int32, NZ)) % NZ
    to_x = (x + lax.iota(jnp.int32, NX)) % NX
    table = jnp.take(jnp.take(table, to_x, axis=0), from_z, axis=2)
    requests = jnp.maximum(jnp.transpose(table, (2, 0, 1)).ravel(), 0)
    held = exchanged(requests, blocks)

    slots = ((z - pair_slots % NZ) % NZ) * NX + (x - pair_slots // NZ) % NX
    summary = correlated(slots, pair_count, held)
    return summary.reshape(summary.shape[0], NW, 2, BLK)


def solution(mesh):
    placed = (P("tm", "asset"), P("asset"), P(), P(("asset", "tm"), None), P(("asset", "tm")))
    return jax.shard_map(
        on_device,
        mesh=mesh,
        in_specs=placed,
        out_specs=P(("asset", "tm"), None, None, None),
        check_vma=False,
    )
```

time: 276 us -> 136 us (0.49)
  Pallas kernels: 0 us -> 116 us
  waiting for transfers between devices: 105 us -> 0.01 us
  matrix products: 71.8 us -> 3.19 us
  local copies, waits for them, and re-layouts: 48.3 us -> 7.9 us
  other arithmetic: 24.1 us -> 3.17 us
  starting transfers between devices: 25 us -> 4.57 us
    pallas_call x0 -> x3, Pallas kernels: none -> 116 us  [the longest x1 63.9 us: exchanged(): pl.pallas_call(exchange_kernel, out_shape=jax.ShapeDtypeStruct((NZ, NT, N...]
    all_to_all x2 -> x0, waiting for transfers between devices: 105 us -> none  [the longest x1 96 us: exchange_both(): parts = lax.all_to_all(parts, axis, split_axis=0, concat_axis=0, tiled=True)]
    dot_general x6 -> x1, matrix products: 70.2 us -> 1.62 us  [on_device(): totals = jnp.dot(returns, member, precision=highest)]
    gather x6 -> x2, local copies, waits for them, and re-layouts: 23.6 us -> 1.12 us  [on_device(): table = jnp.take(jnp.take(table, to_x, axis=0), from_z, axis=2)]
    all_to_all x2 -> x0, starting transfers between devices: 20.4 us -> none  [the longest x1 11 us: copy_for_each(): lax.all_to_all(jnp.broadcast_to(array[None], (devices, *array.shape)), ax...]
    select_n x4 -> x3, other arithmetic: 18.9 us -> 0.1 us  [on_device(): table = jnp.take(jnp.take(table, to_x, axis=0), from_z, axis=2)]
    another operation x7 -> x0, local copies, waits for them, and re-layouts: 9.8 us -> none  [the longest x1 5.5 us: on_device(): series = arrived.reshape(arrived.shape[0], arrived.shape[1], BLK)]
    all_to_all x1 -> x0, local copies, waits for them, and re-layouts: 4.72 us -> none  [exchange_both(): parts = lax.all_to_all(parts, axis, split_axis=0, concat_axis=0, tiled=True)]
  transfers between devices with their start and end apart: 3 -> 1, of which waited for: 2 -> 0; matrix products, arithmetic and copies ran while one was open for 1% -> 4% of each run, Pallas kernels for 0% -> 0%
where the time goes in v1:
time: 136 us; the launch traced here: 135 us
  Pallas kernels  116 us (85%)
  local copies, waits for them, and re-layouts  7.9 us (6%)
  starting transfers between devices  4.57 us (3%)
  matrix products  3.19 us (2%)
  other arithmetic  3.17 us (2%)
    pallas_call x1, Pallas kernels, exchanged(): pl.pallas_call(exchange_kernel, out_shape=jax.ShapeDtypeStruct((NZ, NT, N...  63.9 us
    pallas_call x1, Pallas kernels, correlated(): pl.pallas_call(pair_kernel, out_shape=jax.ShapeDtypeStruct((pairs, 2 * NW...  36.2 us
    pallas_call x1, Pallas kernels, summed(): pl.pallas_call(total_kernel, out_shape=jax.ShapeDtypeStruct(message.shape...  15.7 us
    ppermute x1, starting transfers between devices, shifted(): return lax.ppermute(block, axis, route)  4.57 us
  transfers between devices with their start and end apart: 1, of which 0 were waited for; matrix products, arithmetic and copies ran while one was open for 4% of the time, Pallas kernels for 0%

profile of v1, /device:TPU:1, one launch (start us, length us, event | category | flops | bytes accessed | tf_op | source)
XLA Modules:
  0.0 135.4 jit_solution(10609207048719973989)
XLA Ops:
  0.0 0.8 slice.12
  0.8 4.6 %collective-permute-start = (f32[1,1920]{1,0:T(1,128)S(1)}, f32[1,1920]{1,0:T(1,128)S(1)}, u32[]{:S(2)}, u32[]{:S(2)}) collective-permute-start(f32[1,1920]{1,0:T(1,128)S(1)} %slice.12), channel_id=1, source_target_pairs={{0,1},{1,2},{2,3},{3,4},{4,5},{5,6},{6,7},{8,9},{9,10},{10,11},{11... | collective-permute-start | bytes 23048 | tf_op jit(solution)/shard_map/ppermute | solution.py:28
  5.5 0.7 broadcast_compare_fusion
  6.2 0.8 copy.34
  7.0 0.8 convert_reduce_fusion
  7.9 0.1 copy.37
  8.0 1.2 reshape.141
  9.2 0.6 gather_fusion
  9.8 0.1 broadcast_select_fusion
  9.8 0.1 copy.41
  9.9 0.8 fusion.6.slots
  10.7 0.6 gather_fusion.1
  11.2 0.1 select_maximum_fusion
  12.0 0.1 max.13.requests
  12.1 1.6 %fusion.2 = f32[60,11]{1,0:T(8,128)S(1)} fusion(s32[1920]{0:T(1024)} %param.6, f32[60,1920]{1,0:T(8,128)} %param.5, f32[59,1920]{1,0:T(8,128)} %bitcast.20, f32[1,1920]{1,0:T(1,128)S(1)} %collective-permute-done, pred[60]{0:T(512)(128)(4,1)S(1)} %add_compare_fusion), kind=kOutput, calls=%fused_computation.10 | convolution fusion | flops 15573120 | bytes 931980 | tf_op jit(solution)/shard_map/dot_general | solution.py:402
  13.7 0.1 reshape.142
  13.9 0.7 fusion.15.message
  14.5 15.7 %shard_map.55 = f32[8,128]{1,0:T(8,128)} custom-call(f32[8,128]{1,0:T(8,128)} %fusion.15.message), custom_call_target="tpu_custom_call" | custom-call | tf_op jit(solution)/shard_map/pallas_call | solution.py:60
  30.2 0.8 slice.15
  30.9 0.8 reshape.145
  31.7 1.6 %fusion = bf16[60,1920]{1,0:T(8,128)(2,1)S(1)} fusion(s32[1920]{0:T(1024)} %param.6, f32[60,11]{1,0:T(8,128)S(1)} %reshape.145, f32[11]{0:T(128)S(1)} %slice.15, f32[60,1920]{1,0:T(8,128)} %param.5, f32[59,1920]{1,0:T(8,128)} %bitcast.21, f32[1,1920]{1,0:T(1,128)S(1)} %collective-permute-done, pred[60]{0:T(512)(128)(4,1)S(1)} %add_compare_fusion), kind=kOutput, calls=%fused_computation.3 | convolution fusion | flops 15804180 | bytes 1162424 | tf_op jit(solution)/shard_map/dot_general | solution.py:410
  33.4 63.9 %shard_map.56.held = bf16[8,8,4,64,128]{4,3,2,1,0:T(8,128)(2,1)S(1)} custom-call(s32[256]{0:T(256)S(1)} %max.13.requests, bf16[15,64,128]{2,1,0:T(8,128)(2,1)S(1)} %bitcast_bitcast_fusion.blocks), custom_call_target="tpu_custom_call" | custom-call | tf_op jit(solution)/shard_map/pallas_call | solution.py:205
  97.3 1.9 %copy-done = bf16[8,8,4,64,128]{4,3,2,1,0:T(8,128)(2,1)} copy-done((bf16[8,8,4,64,128]{4,3,2,1,0:T(8,128)(2,1)}, bf16[8,8,4,64,128]{4,3,2,1,0:T(8,128)(2,1)S(1)}, u32[]{:S(2)}) %copy-start) | copy-done | bytes 4194328
  99.2 36.2 %shard_map.57 = f32[128,8,128]{2,1,0:T(8,128)} custom-call(s32[128,2]{1,0:T(8,128)} %fusion.6.slots, s32[1]{0:T(128)S(6)} %copy.56.used, bf16[8,8,4,64,128]{4,3,2,1,0:T(8,128)(2,1)} %copy-done), custom_call_target="tpu_custom_call" | custom-call | tf_op jit(solution)/shard_map/pallas_call | solution.py:369
  (11 shorter events, 0.2 us)
Async XLA Ops:
  0.8 11.2 %collective-permute-start = (f32[1,1920]{1,0:T(1,128)S(1)}, f32[1,1920]{1,0:T(1,128)S(1)}, u32[]{:S(2)}, u32[]{:S(2)}) collective-permute-start(f32[1,1920]{1,0:T(1,128)S(1)} %slice.12), channel_id=1, source_target_pairs={{0,1},{1,2},{2,3},{3,4},{4,5},{5,6},{6,7},{8,9},{9,10},{10,11},{11... | collective-permute-start | bytes 23048 | tf_op jit(solution)/shard_map/ppermute | solution.py:28
  97.3 1.9 %copy-start = (bf16[8,8,4,64,128]{4,3,2,1,0:T(8,128)(2,1)}, bf16[8,8,4,64,128]{4,3,2,1,0:T(8,128)(2,1)S(1)}, u32[]{:S(2)}) copy-start(bf16[8,8,4,64,128]{4,3,2,1,0:T(8,128)(2,1)S(1)} %shard_map.56.held) | copy-start | bytes 12582916

commit v2 on v1

v2 whole, which is shorter than its diff:
```python
import functools

import jax
import jax.numpy as jnp
from jax import lax
from jax.experimental import pallas as pl
from jax.experimental.pallas import tpu as pltpu
from jax.sharding import PartitionSpec as P

BLK = 128
NX, NZ, NY, NC = 4, 8, 4, 2
NA, NT = NX * NZ, NY * NC
ROWS = 64
MINUTES = 60
HALF = 30
WIN = 390
NW = 4
MESH = pl.DeviceIdType.MESH

epsilon = 1e-06


def shifted(block, axis, distance):
    devices = range(lax.axis_size(axis))
    route = [(i - distance, i) for i in devices if i - distance in devices]
    return lax.ppermute(block, axis, route)


def three_parts(value):
    high = value.astype(jnp.bfloat16).astype(jnp.float32)
    rest = value - high
    middle = rest.astype(jnp.bfloat16).astype(jnp.float32)
    low = (rest - middle).astype(jnp.bfloat16).astype(jnp.float32)
    return high, middle, low


def front_kernel(
    prices, previous, sectors, blocks, mine, line, from_x, from_z, x_send, x_recv, z_send, z_recv
):
    d = lax.axis_index("asset")
    t = lax.axis_index("tm")
    x, z = d // NZ, d % NZ
    x_peers = [((x + k) % NX) * NZ + z for k in range(1, NX)]
    z_peers = [x * NZ + (z + k) % NZ for k in range(1, NZ)]
    barrier = pltpu.get_barrier_semaphore()
    for peer in x_peers + z_peers:
        pl.semaphore_signal(barrier, inc=1, device_id=(peer, t), device_id_type=MESH)

    width = prices.shape[1]
    labels = 16
    price = prices[...]
    earlier = jnp.concatenate([previous[...], price[: MINUTES - 1]], axis=0)
    row = lax.broadcasted_iota(jnp.int32, (MINUTES, width), 0)
    returns = jnp.where((row == 0) & (t == 0), 0.0, price - earlier)
    spare = lax.broadcasted_iota(jnp.int32, (ROWS - MINUTES, width), 0)
    ones = jnp.where(spare == 0, 1.0, 0.0)
    parts = three_parts(jnp.concatenate([returns, ones], axis=0))
    label = lax.broadcasted_iota(jnp.int32, (labels, width), 0)
    member = jnp.where(label == sectors[...], 1.0, 0.0).astype(jnp.bfloat16)
    totals = jnp.zeros((labels, ROWS), jnp.float32)
    for part in parts:
        totals = totals + lax.dot_general(
            member,
            part.astype(jnp.bfloat16),
            (((1,), (1,)), ((), ())),
            preferred_element_type=jnp.float32,
        )
    mine[...] = jnp.concatenate([totals[:8], totals[8:]], axis=1)
    pl.semaphore_wait(barrier, len(x_peers) + len(z_peers))

    def gather(source, slots, peers, send_sem, recv_sem):
        copies = []
        for k, peer in enumerate(peers):
            copy = pltpu.make_async_remote_copy(
                src_ref=source,
                dst_ref=slots.at[k],
                send_sem=send_sem.at[k],
                recv_sem=recv_sem.at[k],
                device_id=(peer, t),
                device_id_type=MESH,
            )
            copy.start()
            copies.append(copy)
        for copy in copies:
            copy.wait_recv()
        total = source[...]
        for k in range(len(peers)):
            total = total + slots[k]
        return total, copies

    total, sent = gather(mine, from_x, x_peers, x_send, x_recv)
    line[...] = total
    total, more = gather(line, from_z, z_peers, z_send, z_recv)
    totals = jnp.concatenate([total[:, :ROWS], total[:, ROWS:]], axis=0)
    members = totals[:, MINUTES : MINUTES + 1]
    mean = totals / jnp.where(members > 0, members, 1.0)
    parts = jnp.concatenate(three_parts(mean), axis=0)
    parts = jnp.concatenate([parts, jnp.zeros((BLK - 3 * labels, ROWS), jnp.float32)], axis=0)
    parts = jnp.concatenate([parts, jnp.zeros((BLK, BLK - ROWS), jnp.float32)], axis=1)
    by_minute = jnp.transpose(parts)[:ROWS, : 3 * labels].astype(jnp.bfloat16)
    members3 = jnp.concatenate([member, member, member], axis=0)
    common = jnp.dot(by_minute, members3, preferred_element_type=jnp.float32)
    neutral = jnp.concatenate([returns, ones], axis=0) - common
    for n in range(width // BLK):
        blocks[n] = neutral[:, n * BLK : (n + 1) * BLK].astype(jnp.bfloat16)
    for copy in sent + more:
        copy.wait_send()


def neutral_blocks(prices, previous, sectors):
    return pl.pallas_call(
        front_kernel,
        out_shape=jax.ShapeDtypeStruct((prices.shape[1] // BLK, ROWS, BLK), jnp.bfloat16),
        in_specs=[pl.BlockSpec(memory_space=pltpu.VMEM)] * 3,
        out_specs=pl.BlockSpec(memory_space=pltpu.VMEM),
        scratch_shapes=[
            pltpu.VMEM((8, BLK), jnp.float32),
            pltpu.VMEM((8, BLK), jnp.float32),
            pltpu.VMEM((NX - 1, 8, BLK), jnp.float32),
            pltpu.VMEM((NZ - 1, 8, BLK), jnp.float32),
            pltpu.SemaphoreType.DMA((NX - 1,)),
            pltpu.SemaphoreType.DMA((NX - 1,)),
            pltpu.SemaphoreType.DMA((NZ - 1,)),
            pltpu.SemaphoreType.DMA((NZ - 1,)),
        ],
        compiler_params=pltpu.CompilerParams(collective_id=0, has_side_effects=True),
    )(prices, previous, sectors)


ORDER = (0, 1, 7, 2, 6, 3, 5, 4)
FIRST_HALF = 8
PLACE = (0, 1, 3, 2)


def exchange_kernel(
    requests, blocks, out, g1, g2, g3, g4, g5, g6, g7, picked, relay,
    z_send, z_recv, x_send, x_recv, y_send, y_recv, own_sem,
):
    d = lax.axis_index("asset")
    t = lax.axis_index("tm")
    x, z, y, c = d // NZ, d % NZ, t // NC, t % NC
    gathered = (blocks, g1, g2, g3, g4, g5, g6, g7)
    count = blocks.shape[0]
    minutes = pl.ds(0, MINUTES)

    def at_x(k):
        return ((x + k) % NX) * NZ + z, t

    def at_z(k):
        return x * NZ + (z + k + NZ) % NZ, t

    others = [(dy, dc) for dy in (1, 3, 2, 0) for dc in (0, 1) if (dy, dc) != (0, 0)]

    def at_y(k, sign):
        dy, dc = others[k]
        return d, ((y + sign * dy + NY) % NY) * NC + (c + dc) % NC

    barrier = pltpu.get_barrier_semaphore()
    peers = [at_z(1), at_z(-1)] + [at_x(k) for k in range(1, NX)]
    peers += [at_y(k, 1) for k in range(len(others))]
    for peer in peers:
        pl.semaphore_signal(barrier, inc=1, device_id=peer, device_id_type=MESH)

    pending = []

    def along_z(source, target, number, first, size, step):
        copy = pltpu.make_async_remote_copy(
            src_ref=gathered[source].at[pl.ds(first, size), minutes],
            dst_ref=gathered[target].at[pl.ds(first, size), minutes],
            send_sem=z_send.at[number],
            recv_sem=z_recv.at[number],
            device_id=at_z(step),
            device_id_type=MESH,
        )
        copy.start()
        pending.append(copy)
        return copy

    def pick(j):
        column = x * NZ + (z + NZ - j) % NZ
        for k in (1, 3, 2, 0):
            def one(i, _):
                block = gathered[j][jnp.maximum(requests[(x + k) % NX, i, column], 0)]
                if k == 0:
                    relay[j, i, PLACE[0]] = block
                else:
                    picked[j, k - 1, i] = block
                return 0
            lax.fori_loop(0, NT, one, 0)

    def along_x(j):
        copies = []
        for k in (1, 3, 2):
            copy = pltpu.make_async_remote_copy(
                src_ref=picked.at[j, k - 1, :, minutes],
                dst_ref=relay.at[j, :, PLACE[k], minutes],
                send_sem=x_send.at[j, k],
                recv_sem=x_recv.at[j, k],
                device_id=at_x(k),
                device_id_type=MESH,
            )
            copy.start()
            copies.append(copy)
        pending.extend(copies)
        return copies

    def along_y(j, arriving):
        copies = []
        for part, (first, size) in enumerate(((0, NX - 1), (NX - 1, 1))):
            for copy in arriving[:2] if part == 0 else arriving[2:]:
                copy.wait_recv()
            places = pl.ds(first, size)
            for k in range(len(others)):
                target = at_y(k, 1)
                copy = pltpu.make_async_remote_copy(
                    src_ref=relay.at[j, target[1], places, minutes],
                    dst_ref=out.at[j, t, places, minutes],
                    send_sem=y_send.at[j, part, k],
                    recv_sem=y_recv.at[j, part, k],
                    device_id=target,
                    device_id_type=MESH,
                )
                copy.start()
                copies.append(copy)
        pending.extend(copies)
        own = pltpu.make_async_copy(relay.at[j, t], out.at[j, t], own_sem.at[j])
        own.start()
        return copies, own

    pick(ORDER[0])
    pl.semaphore_wait(barrier, len(peers))
    arrivals = {}
    arrivals[1] = [along_z(0, 1, 1, 0, count, 1)]
    arrivals[7] = [along_z(0, 7, 7, 0, count, -1)]
    crossing = {}
    landing = []
    previous = None
    for j in ORDER:
        for copy in arrivals.get(j, ()):
            copy.wait_recv()
        if j in (1, 2):
            arrivals[j + 1] = [along_z(j, j + 1, j + 1, 0, count, 1)]
        if j in (7, 6):
            arrivals[j - 1] = [along_z(j, j - 1, j - 1, 0, count, -1)]
        if j == 3:
            arrivals[4] = [along_z(3, 4, 4, 0, FIRST_HALF, 1)]
        if j == 5:
            arrivals[4].append(along_z(5, 4, 0, FIRST_HALF, count - FIRST_HALF, -1))
        if j != ORDER[0]:
            pick(j)
        crossing[j] = along_x(j)
        if previous is not None:
            landing.append(along_y(previous, crossing[previous]))
        previous = j
    landing.append(along_y(previous, crossing[previous]))
    for copies, own in landing:
        for copy in copies:
            copy.wait_recv()
        own.wait()
    for copy in pending:
        copy.wait_send()


def exchanged(requests, blocks):
    count = blocks.shape[0]
    block = blocks.shape[1:]
    gathered = [pltpu.VMEM((count, *block), blocks.dtype) for _ in range(NZ - 1)]
    return pl.pallas_call(
        exchange_kernel,
        out_shape=jax.ShapeDtypeStruct((NZ, NT, NX, *block), blocks.dtype),
        in_specs=[
            pl.BlockSpec(memory_space=pltpu.SMEM),
            pl.BlockSpec(memory_space=pltpu.VMEM),
        ],
        out_specs=pl.BlockSpec(memory_space=pl.ANY),
        scratch_shapes=gathered
        + [
            pltpu.VMEM((NZ, NX - 1, NT, *block), blocks.dtype),
            pltpu.VMEM((NZ, NT, NX, *block), blocks.dtype),
            pltpu.SemaphoreType.DMA((NZ,)),
            pltpu.SemaphoreType.DMA((NZ,)),
            pltpu.SemaphoreType.DMA((NZ, NX)),
            pltpu.SemaphoreType.DMA((NZ, NX)),
            pltpu.SemaphoreType.DMA((NZ, 2, NT)),
            pltpu.SemaphoreType.DMA((NZ, 2, NT)),
            pltpu.SemaphoreType.DMA((NZ,)),
        ],
        compiler_params=pltpu.CompilerParams(
            collective_id=1, has_side_effects=True, vmem_limit_bytes=40 * 2**20
        ),
    )(requests, blocks)


def pair_kernel(
    slots, used, held, out, near, left, right, inverse, spread, columns, product0, product1, sem
):
    loads = [pltpu.make_async_copy(held.at[j], near.at[j], sem.at[j]) for j in range(NZ)]
    for load in loads:
        load.start()
    tile = 16
    row = lax.broadcasted_iota(jnp.int32, (tile, BLK), 0)
    zero = jnp.zeros((tile, BLK), jnp.float32)
    tiles = ROWS // tile
    spare = MINUTES - (tiles - 1) * tile

    def folded(parts):
        total = parts[0]
        for part in parts[1:]:
            total = total + part
        return total[:8] + total[8:]

    def both(parts):
        return folded(parts), folded([part * part for part in parts])

    def with_rows(tail, values):
        for n, value in enumerate(values):
            tail = jnp.where(row == spare + n, jnp.broadcast_to(value, (tile, BLK)), tail)
        return tail

    def prepare(j, k):
        slot = j * NX + k
        packed, wide = [], []
        for i in range(NT):
            whole = near[j, i, k]
            packed.append([whole[tile * q : tile * q + tile] for q in range(tiles)])
            wide.append([part.astype(jnp.float32) for part in packed[i]])
            wide[i][-1] = jnp.where(row < spare, wide[i][-1], zero)
            packed[i][-1] = wide[i][-1].astype(jnp.bfloat16)
        blank = zero.astype(jnp.bfloat16)
        cut = HALF - tile
        halves = {}
        for i in (0, 1, 6, 7):
            early = jnp.where(row < cut, wide[i][1], zero)
            late = jnp.where(row < cut, zero, wide[i][1])
            halves[i, 0] = both([wide[i][0], early])
            halves[i, 1] = both([late] + wide[i][2:])
            if i < 2:
                packed.append([blank, late.astype(jnp.bfloat16)] + packed[i][2:])
            else:
                packed.append([packed[i][0], early.astype(jnp.bfloat16), blank, blank])
        late0, late1, early6, early7 = packed[NT:]
        none = [blank] * tiles
        kept = [
            [packed[0], packed[1]] + packed[2:6] + [early6, none],
            [late0, packed[1]] + packed[2:6] + [packed[6], none],
            [none, packed[1]] + packed[2:6] + [packed[6], early7],
            [none, late1] + packed[2:6] + [packed[6], packed[7]],
        ]
        middle = both([part for i in range(2, 6) for part in wide[i]])
        inside = [middle[n] + halves[1, 1][n] + halves[6, 0][n] for n in range(2)]
        extra = (
            ((0, 0), (0, 1), (1, 0)),
            ((0, 1), (1, 0), (6, 1)),
            ((1, 0), (6, 1), (7, 0)),
            ((6, 1), (7, 0), (7, 1)),
        )
        weights, lefts, rights = [], [], []
        for w in range(NW):
            first, second = inside
            for part in extra[w]:
                first = first + halves[part][0]
                second = second + halves[part][1]
            first = jnp.sum(first, axis=0, keepdims=True)
            second = jnp.sum(second, axis=0, keepdims=True)
            center = first / WIN
            variance = second / WIN - center * center
            weights.append(1.0 / (variance + epsilon))
            h, m, l = three_parts(-first)
            lefts += [h, h, m, h, l, m, m, l]
            h, m, l = three_parts(center)
            rights += [h, m, h, l, h, m, l, m]
        inverse[slot] = jnp.concatenate(weights + weights, axis=0)
        for w in range(NW):
            spread[slot, w] = jnp.transpose(jnp.broadcast_to(weights[w], (BLK, BLK)))
        rest = ROWS - MINUTES
        for w in range(NW):
            for i in range(NT):
                parts = list(kept[w][i])
                if i // 2 == w:
                    tail = parts[-1].astype(jnp.float32)
                    parts[-1] = with_rows(tail, rights[rest * i : rest * i + rest]).astype(jnp.bfloat16)
                for q in range(tiles):
                    right[slot, pl.ds(i * ROWS + tile * q, tile), pl.ds(w * BLK, BLK)] = parts[q]
        for i in range(0, NT, 2):
            parts = []
            for n in (i, i + 1):
                tail = with_rows(wide[n][-1], lefts[rest * n : rest * n + rest])
                parts += wide[n][:-1] + [tail]
            left[slot, :, pl.ds(i * ROWS, 2 * ROWS)] = jnp.transpose(jnp.concatenate(parts, axis=0)).astype(jnp.bfloat16)
        return j

    def arrive(j, _):
        pltpu.make_async_copy(held.at[j], near.at[j], sem.at[j]).wait()
        for k in range(NX):
            prepare(j, k)
        return 0

    lax.fori_loop(0, NZ, arrive, 0)

    pairs = out.shape[0]
    products = (product0, product1)
    group = BLK // NW
    lane8 = lax.broadcasted_iota(jnp.int32, (8, BLK), 1)
    scale = 1.0 / (WIN * BLK)

    def multiply(p, product, half):
        a, b = slots[0, p], slots[1, p]
        part = pl.ds(2 * half * BLK, 2 * BLK)
        product[:, part] = jnp.dot(left[a], right[b, :, part], preferred_element_type=jnp.float32)

    def reduce(p, product, half):
        a, b = slots[0, p], slots[1, p]
        within = lax.rem(p, group) * NW
        windows = (2 * half, 2 * half + 1)
        weight = {w: inverse[b, pl.ds(w, 1)] for w in windows}
        total = {w: jnp.zeros((8, BLK), jnp.float32) for w in windows}
        for i in range(BLK // 8):
            rows = pl.ds(8 * i, 8)
            keep = columns[rows, :]
            for w in windows:
                value = product[rows, pl.ds(w * BLK, BLK)]
                scaled = value * value * spread[a, w, rows]
                total[w] = total[w] + scaled
                over_j = jnp.sum(scaled * weight[w], axis=1, keepdims=True)
                keep = jnp.where(lane8 == within + w, over_j, keep)
            columns[rows, :] = keep
        for w in windows:
            over_i = jnp.sum(total[w], axis=0, keepdims=True) * (weight[w] * scale)
            out[p, pl.ds(2 * w + 1, 1)] = jnp.where(p < used[0], over_i, 0.0)

    def block(n, _):
        def several(m, _):
            p = n * group + 8 * m
            for u in range(8):
                after = p + u + 1 if u < 7 else jnp.minimum(p + 8, pairs - 1)
                for half in range(2):
                    multiply(after, products[1 - u % 2], half)
                    reduce(p + u, products[u % 2], half)
            return 0

        lax.fori_loop(0, group // 8, several, 0)
        turned = jnp.transpose(columns[...]) * scale
        number = lax.broadcasted_iota(jnp.int32, (BLK, BLK), 0) // NW + n * group
        turned = jnp.where(number < used[0], turned, 0.0).reshape(group, NW, BLK)
        for w in range(NW):
            out[pl.ds(n * group, group), 2 * w, :] = turned[:, w, :]
        return 0

    columns[...] = jnp.zeros_like(columns)
    for half in range(2):
        multiply(0, product0, half)
    lax.fori_loop(0, pairs // group, block, 0)


def correlated(slots, used, held):
    pairs = slots.shape[1]
    minutes = NT * ROWS
    return pl.pallas_call(
        pair_kernel,
        out_shape=jax.ShapeDtypeStruct((pairs, 2 * NW, BLK), jnp.float32),
        in_specs=[
            pl.BlockSpec(memory_space=pltpu.SMEM),
            pl.BlockSpec(memory_space=pltpu.SMEM),
            pl.BlockSpec(memory_space=pltpu.HBM),
        ],
        out_specs=pl.BlockSpec(memory_space=pltpu.VMEM),
        scratch_shapes=[
            pltpu.VMEM(held.shape, held.dtype),
            pltpu.VMEM((NA, BLK, minutes), jnp.bfloat16),
            pltpu.VMEM((NA, minutes, NW * BLK), jnp.bfloat16),
            pltpu.VMEM((NA, 8, BLK), jnp.float32),
            pltpu.VMEM((NA, NW, BLK, BLK), jnp.float32),
            pltpu.VMEM((BLK, BLK), jnp.float32),
            pltpu.VMEM((BLK, NW * BLK), jnp.float32),
            pltpu.VMEM((BLK, NW * BLK), jnp.float32),
            pltpu.SemaphoreType.DMA((NZ,)),
        ],
        compiler_params=pltpu.CompilerParams(vmem_limit_bytes=56 * 2**20),
    )(slots, used, held)


def on_device(prices, sectors, wanted, pair_slots, pair_count):
    stretch = prices.shape[0]
    column_index = lax.axis_index("asset")
    x, z = column_index // NZ, column_index % NZ
    previous = shifted(prices[stretch - 1 :], "tm", 1)
    blocks = neutral_blocks(prices, previous, sectors.reshape(1, -1))

    requests = lax.dynamic_index_in_dim(wanted.reshape(NX, NZ, NT, NA), z, 1, keepdims=False)
    held = exchanged(requests, blocks)

    across = (x - pair_slots // NZ) % NX
    across = jnp.where(across > 1, 5 - across, across)
    slots = (((z - pair_slots) % NZ) * NX + across).T
    summary = correlated(slots, pair_count, held)
    return summary.reshape(summary.shape[0], NW, 2, BLK)


def solution(mesh):
    placed = (P("tm", "asset"), P("asset"), P(), P(("asset", "tm"), None), P(("asset", "tm")))
    return jax.shard_map(
        on_device,
        mesh=mesh,
        in_specs=placed,
        out_specs=P(("asset", "tm"), None, None, None),
        check_vma=False,
    )
```

time: 136 us -> 113 us (0.83)
  Pallas kernels: 116 us -> 100 us
  matrix products: 3.19 us -> 0 us
  local copies, waits for them, and re-layouts: 7.9 us -> 5.64 us
  other arithmetic: 3.17 us -> 1.28 us
    pallas_call x1, Pallas kernels: 36.2 us -> 24 us  [correlated(): pl.pallas_call(pair_kernel, out_shape=jax.ShapeDtypeStruct((pairs, 2 * NW...]
    pallas_call x1, Pallas kernels: 63.9 us -> 59.7 us  [exchanged(): pl.pallas_call(exchange_kernel, out_shape=jax.ShapeDtypeStruct((NZ, NT, N...]
    dot_general x2 -> x0, matrix products: 3.19 us -> none  [the longest x1 1.62 us: on_device(): totals = jnp.dot(returns, member, precision=highest)]
    unnamed x3 -> x8, local copies, waits for them, and re-layouts: 2.7 us -> 3.47 us
  transfers between devices with their start and end apart: 1 -> 1, of which waited for: 0 -> 0; matrix products, arithmetic and copies ran while one was open for 4% -> 2% of each run, Pallas kernels for 0% -> 0%
where the time goes in v2:
time: 113 us; the launch traced here: 112 us
  Pallas kernels  100 us (88%)
  local copies, waits for them, and re-layouts  5.64 us (5%)
  starting transfers between devices  4.57 us (4%)
  other arithmetic  1.28 us (1%)
    pallas_call x1, Pallas kernels, exchanged(): pl.pallas_call(exchange_kernel, out_shape=jax.ShapeDtypeStruct((NZ, NT, N...  59.7 us
    pallas_call x1, Pallas kernels, correlated(): pl.pallas_call(pair_kernel, out_shape=jax.ShapeDtypeStruct((pairs, 2 * NW...  24 us
    pallas_call x1, Pallas kernels, neutral_blocks(): pl.pallas_call(front_kernel, out_shape=jax.ShapeDtypeStruct((prices.shape...  16.5 us
    ppermute x1, starting transfers between devices, shifted(): return lax.ppermute(block, axis, route)  4.57 us
    unnamed x8, local copies, waits for them, and re-layouts  3.47 us
  transfers between devices with their start and end apart: 1, of which 0 were waited for; matrix products, arithmetic and copies ran while one was open for 2% of the time, Pallas kernels for 0%

profile of v2, /device:TPU:1, one launch (start us, length us, event | category | flops | bytes accessed | tf_op | source)
XLA Modules:
  0.0 112.4 jit_solution(4835494320059136419)
XLA Ops:
  0.0 0.0 copy-start
  0.0 0.9 slice.3
  0.9 4.6 %collective-permute-start = (f32[1,1920]{1,0:T(1,128)S(1)}, f32[1,1920]{1,0:T(1,128)S(1)}, u32[]{:S(2)}, u32[]{:S(2)}) collective-permute-start(f32[1,1920]{1,0:T(1,128)S(1)} %slice.3), channel_id=1, source_target_pairs={{0,1},{1,2},{2,3},{3,4},{4,5},{5,6},{6,7},{8,9},{9,10},{10,11},{11... | collective-permute-start | bytes 23048 | tf_op jit(solution)/shard_map/ppermute | solution.py:26
  5.5 1.3 %fusion.4.slots = s32[2,128]{1,0:T(2,128)} fusion(s32[128,2]{0,1:T(2,128)} %param.8, s32[]{:T(128)S(6)} %select_n.35, s32[]{:T(128)S(6)} %select_n.33), kind=kLoop, calls=%fused_computation.16 | loop fusion | flops 11264 | bytes 2056 | tf_op jit(solution)/shard_map/transpose | solution.py:494
  6.8 0.0 copy-done
  7.4 1.3 %reshape.10.sectors = s32[1,1920]{1,0:T(1,128)} reshape(s32[1920]{0:T(1024)} %param.6) | data formatting | bytes 15360 | tf_op jit(solution)/shard_map/reshape | solution.py:487
  8.7 0.0 collective-permute-done.previous
  8.7 0.0 copy-start.3
  8.7 0.6 copy-done.3
  9.3 16.5 %shard_map.55.blocks = bf16[15,64,128]{2,1,0:T(8,128)(2,1)} custom-call(f32[60,1920]{1,0:T(8,128)} %prices.1, f32[1,1920]{1,0:T(1,128)} %copy-done.3, s32[1,1920]{1,0:T(1,128)} %reshape.10.sectors), custom_call_target="tpu_custom_call" | custom-call | tf_op jit(solution)/shard_map/pallas_call | solution.py:111
  25.8 0.0 copy-start.2
  25.8 0.9 copy-done.2
  26.7 59.7 %shard_map.56.held = bf16[8,8,4,64,128]{4,3,2,1,0:T(8,128)(2,1)S(1)} custom-call(s32[4,8,32]{2,1,0:T(8,128)S(1)} %dynamic-slice_bitcast_fusion.requests, bf16[15,64,128]{2,1,0:T(8,128)(2,1)S(1)} %copy-done.2), custom_call_target="tpu_custom_call" | custom-call | tf_op jit(solution)/shard_map/pallas_call | solution.py:268
  86.4 0.0 copy-start.1
  86.4 1.9 %copy-done.1 = bf16[8,8,4,64,128]{4,3,2,1,0:T(8,128)(2,1)} copy-done((bf16[8,8,4,64,128]{4,3,2,1,0:T(8,128)(2,1)}, bf16[8,8,4,64,128]{4,3,2,1,0:T(8,128)(2,1)S(1)}, u32[]{:S(2)}) %copy-start.1) | copy-done | bytes 4194328
  88.4 24.0 %shard_map.57 = f32[128,8,128]{2,1,0:T(8,128)} custom-call(s32[2,128]{1,0:T(2,128)} %fusion.4.slots, s32[1]{0:T(128)S(6)} %copy.8.used, bf16[8,8,4,64,128]{4,3,2,1,0:T(8,128)(2,1)} %copy-done.1), custom_call_target="tpu_custom_call" | custom-call | tf_op jit(solution)/shard_map/pallas_call | solution.py:458
  (1 shorter events, 0.0 us)
Async XLA Ops:
  0.0 6.8 %copy-start = (s32[32,8,32]{2,1,0:T(8,128)S(1)}, s32[32,8,32]{2,1,0:T(8,128)}, u32[]{:S(2)}) copy-start(s32[32,8,32]{2,1,0:T(8,128)} %param.7) | copy-start | bytes 98308
  0.9 7.8 %collective-permute-start = (f32[1,1920]{1,0:T(1,128)S(1)}, f32[1,1920]{1,0:T(1,128)S(1)}, u32[]{:S(2)}, u32[]{:S(2)}) collective-permute-start(f32[1,1920]{1,0:T(1,128)S(1)} %slice.3), channel_id=1, source_target_pairs={{0,1},{1,2},{2,3},{3,4},{4,5},{5,6},{6,7},{8,9},{9,10},{10,11},{11... | collective-permute-start | bytes 23048 | tf_op jit(solution)/shard_map/ppermute | solution.py:26
  8.7 0.6 copy-start.3
  25.8 0.9 copy-start.2
  86.4 1.9 %copy-start.1 = (bf16[8,8,4,64,128]{4,3,2,1,0:T(8,128)(2,1)}, bf16[8,8,4,64,128]{4,3,2,1,0:T(8,128)(2,1)S(1)}, u32[]{:S(2)}) copy-start(bf16[8,8,4,64,128]{4,3,2,1,0:T(8,128)(2,1)S(1)} %shard_map.56.held) | copy-start | bytes 12582916
